TPU v7x, 32 devices: a whole 2x2x4 slice. The times are simulated.
32 devices in a mesh: seq: 8 (over z, y), head: 4 (over x, core).
Axes of the slice: x: 2, y: 2, z: 4, core: 2. Of those that a mesh axis runs over, the one named last changes fastest.
Arguments:
- queries: bfloat16 [1024, 4096], P('seq', 'head'), may hold values from -12 to 12
- keys: bfloat16 [1024, 2048], P('seq', 'head'), may hold values from -12 to 12
- values: bfloat16 [1024, 2048], P('seq', 'head'), may hold values from -6 to 6
- block_order: int32 [16], replicated, may hold values from 0 to 15, each once
Outputs:
- attn: bfloat16 [1024, 4096], P(('seq', 'head'))
- lse: float32 [16, 1024], P('head', 'seq')
Inputs may be any that keep to these rules, and one draw needn't show every extreme that they name: device-order block j (rows j * 64 to j * 64 + 63) holds sequence positions block_order[j] * 64 onward, in order.
All inputs are finite; a program needn't handle non-finite values.
Results may differ from a plain program's by a relative error of at most 0.006.
Values may be sent and summed in bfloat16 or wider, within the bound.
A program may use at most 128 MiB of HBM per device.

v0:
```python
import functools

import jax
import jax.numpy as jnp
from jax import lax
from jax.experimental import pallas as pl
from jax.experimental.pallas import tpu as pltpu
from jax.sharding import PartitionSpec as P

HEAD_SIZE = 256
QUERY_GROUP = 2
MASKED = -1e30
FLOOR = -1e20
PARTS = 2
MESH = pl.DeviceIdType.MESH


def loop(first, last, body):
    if last - first <= 8:
        for i in range(first, last):
            body(i)
    else:
        lax.fori_loop(first, last, lambda i, c: (body(i), c)[1], 0)


def kernel(
    n, nh, order_hbm, q_hbm, k_hbm, v_hbm, attn, lse,
    qbuf, qout, kvown, kvbuf, maxima, sums, accum, obuf, lse_tx, lse_rx, order,
    load_sem, z_send, y_send, kv_recv, q_sem, o_send, o_recv, l_sem,
):
    head_dim, group = HEAD_SIZE, QUERY_GROUP
    rows = k_hbm.shape[0]
    keep = rows // nh
    part = rows // PARTS
    line = n // 2
    scale = head_dim ** (-0.5)
    me, h = lax.axis_index("seq"), lax.axis_index("head")
    p, y = me // 2, lax.rem(me, 2)
    mine = lax.rem(p, 2)
    mate_p = p + 1 - 2 * mine
    mate = mate_p * 2 + y
    across = p * 2 + 1 - y
    width = group * head_dim

    core = lax.rem(h, 2)

    def far(k):
        q, bit = 0, 1
        while bit < line:
            b, c = lax.rem(p // bit, 2), (k // bit) % 2
            q = q + bit * (b + c - 2 * b * c)
            bit *= 2
        return q

    def turn(i):
        i = jnp.int32(i)
        second = jnp.where(i == 1, line - 1, jnp.where(i == 2, 1, line - i + 1))
        return jnp.where(core == 0, second, i)

    def lanes(start, size):
        return pl.ds(pl.multiple_of(start, head_dim), size)

    loads = []

    def load(src, dst):
        c = pltpu.make_async_copy(src, dst, load_sem.at[len(loads)])
        c.start()
        loads.append(c)

    for i, src in enumerate((k_hbm, v_hbm)):
        for t in range(PARTS):
            load(src.at[pl.ds(t * part, part), lanes(mine * head_dim, head_dim)],
                 kvbuf.at[me, t, i])
    for j in range(2):
        for i, src in enumerate((k_hbm, v_hbm)):
            for t in range(PARTS):
                load(src.at[pl.ds(t * part, part), lanes(j * head_dim, head_dim)],
                     kvown.at[j, t, i])
    for g in range(group):
        load(q_hbm.at[:, lanes(((1 - mine) * group + g) * head_dim, head_dim)],
             qout.at[pl.ds(g * rows, rows)])
    for g in range(group):
        load(q_hbm.at[:, lanes((mine * group + g) * head_dim, head_dim)],
             qbuf.at[0, pl.ds(g * rows, rows)])

    load(order_hbm, order)

    barrier = pltpu.get_barrier_semaphore()

    def greet(s, hh):
        pl.semaphore_signal(barrier, inc=1, device_id=(s, hh), device_id_type=MESH)

    greet(across, h)
    loop(1, line, lambda k: greet(far(k) * 2 + y, h))
    for j in range(1, nh):
        greet(me, lax.rem(h + j, nh))
        greet(mate, lax.rem(h + j, nh))

    maxima[...] = jnp.full_like(maxima, FLOOR)
    sums[...] = jnp.zeros_like(sums)
    accum[...] = jnp.zeros_like(accum)

    pl.semaphore_wait(barrier, 1 + (line - 1) + 2 * (nh - 1))

    def y_copy(q, t):
        slot = q * 2 + y
        return pltpu.make_async_remote_copy(
            src_ref=kvbuf.at[slot, t], dst_ref=kvbuf.at[slot, t],
            send_sem=y_send.at[q, t], recv_sem=kv_recv.at[slot, t],
            device_id=(across, h), device_id_type=MESH)

    def z_copy(k, t):
        q = far(k)
        return pltpu.make_async_remote_copy(
            src_ref=kvown.at[lax.rem(q, 2), t], dst_ref=kvbuf.at[me, t],
            send_sem=z_send.at[k, t], recv_sem=kv_recv.at[me, t],
            device_id=(q * 2 + y, h), device_id_type=MESH)

    def landed(slot, t):
        pltpu.make_async_remote_copy(
            src_ref=kvbuf.at[slot, t], dst_ref=kvbuf.at[slot, t],
            send_sem=y_send.at[0, t], recv_sem=kv_recv.at[slot, t],
            device_id=(across, h), device_id_type=MESH).wait_recv()

    def arrived(slot):
        for t in range(PARTS):
            landed(slot, t)

    q_copy = pltpu.make_async_remote_copy(
        src_ref=qout, dst_ref=qbuf.at[1], send_sem=q_sem.at[0], recv_sem=q_sem.at[1],
        device_id=(mate, h), device_id_type=MESH)

    for c in loads[:2 * PARTS]:
        c.wait()
    for t in range(PARTS):
        y_copy(p, t).start()
    for c in loads[2 * PARTS:]:
        c.wait()

    def send(i):
        for t in range(PARTS):
            z_copy(turn(i), t).start()

    send(1)

    @pl.when(core == 1)
    def _():
        q_copy.start()

    loop(2, line, send)

    @pl.when(core == 0)
    def _():
        q_copy.start()

    row = lax.broadcasted_iota(jnp.int32, (rows, rows), 0)
    col = lax.broadcasted_iota(jnp.int32, (rows, rows), 1)
    per = order.shape[0] // n
    blk = rows // per

    def placed(index, s):
        out = index + order[s * per] * blk
        for b in range(1, per):
            out = jnp.where(index >= b * blk, index + (order[s * per + b] - b) * blk, out)
        return out

    query_pos = [placed(row, s) for s in (me, mate)]

    def attend(rs, slot):
        keys, values = kvbuf[slot, :, 0], kvbuf[slot, :, 1]
        keys, values = (z.reshape(rows, head_dim) for z in (keys, values))
        scores = lax.dot_general(
            qbuf[rs], keys, (((1,), (1,)), ((), ())), preferred_element_type=jnp.float32) * scale
        allowed = placed(col, slot) <= query_pos[rs]
        scores = jnp.where(jnp.concatenate([allowed] * group, 0), scores, MASKED)
        before = maxima[rs]
        fresh = jnp.maximum(before, jnp.max(scores, axis=1, keepdims=True))
        weights = jnp.exp(scores - fresh)
        factor = jnp.exp(before - fresh)
        maxima[rs] = fresh
        sums[rs] = sums[rs] * factor + weights
        update = lax.dot_general(
            weights.astype(jnp.bfloat16), values, (((1,), (0,)), ((), ())),
            preferred_element_type=jnp.float32)
        accum[rs] = accum[rs] * jnp.concatenate([factor] * (head_dim // rows), 1) + update

    attend(0, me)
    arrived(across)
    attend(0, across)

    def step(i):
        q = far(turn(i))
        slot = q * 2 + y
        for t in range(PARTS):
            landed(slot, t)
            y_copy(q, t).start()
        attend(0, slot)

    def step_with_last(i):
        step(i)
        last = far(turn(i - 1)) * 2 + 1 - y
        arrived(last)
        attend(0, last)

    step(1)
    loop(2, line, step_with_last)
    q_copy.wait_recv()
    attend(1, me)
    attend(1, across)

    def catch_up(i):
        q = far(turn(i))
        attend(1, q * 2 + y)
        attend(1, q * 2 + 1 - y)

    loop(1, line - 1, catch_up)
    end = far(turn(line - 1))
    attend(1, end * 2 + y)
    final = end * 2 + 1 - y
    arrived(final)

    def finish(rs):
        attend(rs, final)
        total = jnp.sum(sums[rs], axis=1, keepdims=True)
        out = (accum[rs] / total).astype(jnp.bfloat16)
        for g in range(group):
            obuf[rs, :, g * head_dim:(g + 1) * head_dim] = out[g * rows:(g + 1) * rows]
        return jnp.log(total) + maxima[rs]

    def put_lse(rs, full):
        for g in range(group):
            lse_tx[rs, g:g + 1, :] = jnp.transpose(full[g * rows:(g + 1) * rows])[:1]

    columns = lanes((h * 2 + mine) * width, width)

    def o_copy(rs, j):
        to = lax.rem(h + j, nh)
        return pltpu.make_async_remote_copy(
            src_ref=obuf.at[rs, pl.ds(pl.multiple_of(to * keep, keep), keep)],
            dst_ref=attn.at[:, columns],
            send_sem=o_send.at[rs, j], recv_sem=o_recv.at[rs, h],
            device_id=((me, mate)[rs], to), device_id_type=MESH)

    outs = []
    full = finish(1)
    for j in range(nh):
        outs.append(o_copy(1, j))
        outs[-1].start()
    put_lse(1, full)
    lse_copy = pltpu.make_async_remote_copy(
        src_ref=lse_tx.at[1], dst_ref=lse_rx, send_sem=l_sem.at[0], recv_sem=l_sem.at[1],
        device_id=(mate, h), device_id_type=MESH)
    lse_copy.start()
    full = finish(0)
    for j in range(1, nh):
        outs.append(o_copy(0, j))
        outs[-1].start()
    kept = pltpu.make_async_copy(
        obuf.at[0, pl.ds(pl.multiple_of(h * keep, keep), keep)], attn.at[:, columns],
        o_send.at[0, 0])
    kept.start()
    put_lse(0, full)

    lse_copy.wait_recv()
    own, other = lse_tx[0, :group], lse_rx[:group]
    low = jnp.where(mine == 0, own, other)
    high = jnp.where(mine == 0, other, own)
    lse[...] = jnp.concatenate([low, high], 0)

    for rs in range(2):
        for j in range(1 - rs, nh):
            source = lax.rem(h + j, nh)
            spot = lanes((source * 2 + (mine, 1 - mine)[rs]) * width, width)
            pltpu.make_async_remote_copy(
                src_ref=obuf.at[rs, pl.ds(0, keep)], dst_ref=attn.at[:, spot],
                send_sem=o_send.at[rs, j], recv_sem=o_recv.at[rs, source],
                device_id=(mate, h), device_id_type=MESH).wait_recv()
    kept.wait()
    for c in outs:
        c.wait_send()
    lse_copy.wait_send()
    q_copy.wait_send()
    for t in range(PARTS):
        y_copy(p, t).wait_send()
        loop(1, line, lambda k: (z_copy(k, t).wait_send(), y_copy(far(k), t).wait_send()))


def local(n, nh, queries, keys, values, block_order):
    rows = queries.shape[0]
    head_dim, group = HEAD_SIZE, QUERY_GROUP
    line = n // 2
    high = group * rows
    bf16, f32 = jnp.bfloat16, jnp.float32
    dma = pltpu.SemaphoreType.DMA
    return pl.pallas_call(
        functools.partial(kernel, n, nh),
        out_shape=(
            pltpu.VMEM((rows // nh, queries.shape[1] * nh), bf16),
            pltpu.VMEM((2 * group, rows), f32),
        ),
        in_specs=[pl.BlockSpec(memory_space=pl.ANY)] * 4,
        out_specs=(pl.BlockSpec(memory_space=pltpu.VMEM),) * 2,
        scratch_shapes=[
            pltpu.VMEM((2, high, head_dim), bf16),
            pltpu.VMEM((high, head_dim), bf16),
            pltpu.VMEM((2, PARTS, 2, rows // PARTS, head_dim), bf16),
            pltpu.VMEM((n, PARTS, 2, rows // PARTS, head_dim), bf16),
            pltpu.VMEM((2, high, rows), f32),
            pltpu.VMEM((2, high, rows), f32),
            pltpu.VMEM((2, high, head_dim), f32),
            pltpu.VMEM((2, rows, group * head_dim), bf16),
            pltpu.VMEM((2, 8, rows), f32),
            pltpu.VMEM((8, rows), f32),
            pltpu.SMEM(block_order.shape, jnp.int32),
            dma((6 * PARTS + 2 * group + 1,)),
            dma((line, PARTS)),
            dma((line, PARTS)),
            dma((n, PARTS)),
            dma((2,)),
            dma((2, nh)),
            dma((2, nh)),
            dma((2,)),
        ],
        compiler_params=pltpu.CompilerParams(collective_id=0, has_side_effects=True),
    )(block_order, queries, keys, values)


def solution(mesh):
    in_specs = (P("seq", "head"), P("seq", "head"), P("seq", "head"), P())
    out_specs = (P(("seq", "head"), None), P("head", "seq"))
    body = functools.partial(local, mesh.shape["seq"], mesh.shape["head"])
    return jax.shard_map(body, mesh=mesh, in_specs=in_specs, out_specs=out_specs, check_vma=False)
```

profile of v0, /device:TPU:0, one launch (start us, length us, event | category | flops | bytes accessed | tf_op | source)
XLA Modules:
  0.0 29.3 jit_solution(5236477678512006048)
XLA Ops:
  0.6 27.4 %shard_map.59 = (bf16[32,4096]{1,0:T(8,128)(2,1)S(1)}, f32[4,128]{1,0:T(4,128)S(1)}) custom-call(s32[16]{0:T(128)} %order_hbm.1, bf16[128,1024]{1,0:T(8,128)(2,1)} %q_hbm.1, bf16[128,512]{1,0:T(8,128)(2,1)} %k_hbm.1, bf16[128,512]{1,0:T(8,128)(2,1)} %v_hbm.1), custom_call_target="tpu_custom_call" | custom-call | tf_op jit(solution)/shard_map/pallas_call | solution.py:295
  28.0 0.7 %copy.8 = bf16[32,4096]{1,0:T(8,128)(2,1)} copy(bf16[32,4096]{1,0:T(8,128)(2,1)S(1)} %get-tuple-element.2) | data formatting | bytes 524288
  28.7 0.6 %copy.9 = f32[4,128]{1,0:T(4,128)} copy(f32[4,128]{1,0:T(4,128)S(1)} %get-tuple-element.3) | data formatting | bytes 4096
where the time goes:
time: 29.4 us; the launch traced here: 29.3 us
  Pallas kernels  27.4 us (93%)
  local copies, waits for them, and re-layouts  1.28 us (4%)
  between operations  0.64 us (2%)
    pallas_call x1, Pallas kernels, local(): pl.pallas_call(functools.partial(kernel, n, nh), out_shape=(pltpu.VMEM((r...  27.4 us
    unnamed x2, local copies, waits for them, and re-layouts  1.28 us

commit v1 on v0

--- a/solution.py
+++ b/solution.py
@@ -285,6 +285,17 @@
         loop(1, line, lambda k: (z_copy(k, t).wait_send(), y_copy(far(k), t).wait_send()))
 
 
+def hand_over(attn, lse, attn_hbm, lse_hbm, sem):
+    copies = [
+        pltpu.make_async_copy(attn, attn_hbm, sem.at[0]),
+        pltpu.make_async_copy(lse, lse_hbm, sem.at[1]),
+    ]
+    for c in copies:
+        c.start()
+    for c in copies:
+        c.wait()
+
+
 def local(n, nh, queries, keys, values, block_order):
     rows = queries.shape[0]
     head_dim, group = HEAD_SIZE, QUERY_GROUP
@@ -292,7 +303,7 @@
     high = group * rows
     bf16, f32 = jnp.bfloat16, jnp.float32
     dma = pltpu.SemaphoreType.DMA
-    return pl.pallas_call(
+    attn, lse = pl.pallas_call(
         functools.partial(kernel, n, nh),
         out_shape=(
             pltpu.VMEM((rows // nh, queries.shape[1] * nh), bf16),
@@ -323,6 +334,14 @@
         ],
         compiler_params=pltpu.CompilerParams(collective_id=0, has_side_effects=True),
     )(block_order, queries, keys, values)
+    attn, lse = (pltpu.with_memory_space_constraint(z, pltpu.VMEM) for z in (attn, lse))
+    return pl.pallas_call(
+        hand_over,
+        out_shape=(pltpu.HBM(attn.shape, bf16), pltpu.HBM(lse.shape, f32)),
+        in_specs=[pl.BlockSpec(memory_space=pltpu.VMEM)] * 2,
+        out_specs=(pl.BlockSpec(memory_space=pltpu.HBM),) * 2,
+        scratch_shapes=[dma((2,))],
+    )(attn, lse)
 
 
 def solution(mesh):

time: 29.4 us -> 28.9 us (0.983)
  local copies, waits for them, and re-layouts: 1.28 us -> 0 us
  Pallas kernels: 27.4 us -> 28.1 us
    unnamed x2 -> x0, local copies, waits for them, and re-layouts: 1.28 us -> none
    pallas_call x0 -> x1, Pallas kernels: none -> 0.72 us  [local(): pl.pallas_call(hand_over, out_shape=(pltpu.HBM(attn.shape, bf16), pltpu.H...]
where the time goes in v1:
time: 28.9 us; the launch traced here: 28.7 us
  Pallas kernels  28.1 us (97%)
  between operations  0.64 us (2%)
    pallas_call x1, Pallas kernels, local(): pl.pallas_call(functools.partial(kernel, n, nh), out_shape=(pltpu.VMEM((r...  27.4 us
    pallas_call x1, Pallas kernels, local(): pl.pallas_call(hand_over, out_shape=(pltpu.HBM(attn.shape, bf16), pltpu.H...  0.72 us

profile of v1, /device:TPU:0, one launch (start us, length us, event | category | flops | bytes accessed | tf_op | source)
XLA Modules:
  0.0 28.7 jit_solution(11119809271509015330)
XLA Ops:
  0.6 27.4 %shard_map.59 = (bf16[32,4096]{1,0:T(8,128)(2,1)S(1)}, f32[4,128]{1,0:T(4,128)S(1)}) custom-call(s32[16]{0:T(128)} %order_hbm.1, bf16[128,1024]{1,0:T(8,128)(2,1)} %q_hbm.1, bf16[128,512]{1,0:T(8,128)(2,1)} %k_hbm.1, bf16[128,512]{1,0:T(8,128)(2,1)} %v_hbm.1), custom_call_target="tpu_custom_call" | custom-call | tf_op jit(solution)/shard_map/pallas_call | solution.py:306
  28.0 0.7 %shard_map.60 = (bf16[32,4096]{1,0:T(8,128)(2,1)}, f32[4,128]{1,0:T(4,128)}) custom-call(bf16[32,4096]{1,0:T(8,128)(2,1)S(1)} %get-tuple-element.4.attn, f32[4,128]{1,0:T(4,128)S(1)} %get-tuple-element.5.lse), custom_call_target="tpu_custom_call" | custom-call | tf_op jit(solution)/shard_map/pallas_call | solution.py:338

commit v2 on v1

v2 whole, which is shorter than its diff:
```python
import functools

import jax
import jax.numpy as jnp
from jax import lax
from jax.experimental import pallas as pl
from jax.experimental.pallas import tpu as pltpu
from jax.sharding import PartitionSpec as P

HEAD_SIZE = 256
QUERY_GROUP = 2
MASKED = -1e30
FLOOR = -1e20
PARTS = 1
TEAM = 4
MESH = pl.DeviceIdType.MESH


def loop(first, last, body):
    if last - first <= 8:
        for i in range(first, last):
            body(i)
    else:
        lax.fori_loop(first, last, lambda i, c: (body(i), c)[1], 0)


def kernel(
    n, nh, order_hbm, q_hbm, k_hbm, v_hbm, attn, lse,
    qbuf, qout, kvout, kvbuf, maxima, sums, accum, obuf, lse_tx, lse_rx, order,
    load_sem, cross_sem, near_sem, share_sem, kv_recv, q_send, q_recv,
    o_send, o_recv, l_send, l_recv, ready, plane_ready,
):
    head_dim, group = HEAD_SIZE, QUERY_GROUP
    rows = k_hbm.shape[0]
    keep = rows // nh
    part = rows // PARTS
    teams, planes = n // TEAM, nh // 2
    scale = head_dim ** (-0.5)
    width = group * head_dim
    me, h = lax.axis_index("seq"), lax.axis_index("head")
    x, c = h // 2, lax.rem(h, 2)
    g, j = me // TEAM, lax.rem(me, TEAM)
    y = lax.rem(j, 2)
    keeper = 1 - j // 2
    own = c == keeper
    other = jnp.logical_not(own)
    base = 2 * (1 - c)
    partner = x * 2 + 1 - c
    upper = j // 2

    def rank(m):
        return m // 2 + 2 * (m % 2)

    place = upper + 2 * y


    def lanes(start, size):
        return pl.ds(pl.multiple_of(start, head_dim), size)

    barrier = pltpu.get_barrier_semaphore()

    def signal(sem, s, hh):
        pl.semaphore_signal(sem, inc=1, device_id=(s, hh), device_id_type=MESH)

    for m in range(TEAM):
        @pl.when(rank(m) > place)
        def _():
            signal(barrier, g * TEAM + m, x * 2)
            signal(barrier, g * TEAM + m, x * 2 + 1)

    def greet_team(d):
        @pl.when(g + d < teams)
        def _():
            for i in range(2):
                signal(barrier, (g + d) * TEAM + base + i, x * 2 + 1)

            @pl.when(c == 1)
            def _():
                for m in range(TEAM):
                    signal(barrier, (g + d) * TEAM + m, x * 2 + keeper)

    loop(1, teams, greet_team)

    @pl.when(c == 0)
    def _():
        signal(barrier, me, partner)

    for xx in range(planes):
        @pl.when(xx > x)
        def _():
            signal(barrier, me, xx * 2 + c)

    def load(src, dst, i):
        pltpu.make_async_copy(src, dst, load_sem.at[i]).start()

    for i in range(2):
        for g2 in range(group):
            load(q_hbm.at[:, lanes((i * group + g2) * head_dim, head_dim)],
                 qout.at[i, pl.ds(g2 * rows, rows)], 0)
    for i in range(2):
        for t in range(PARTS):
            for z, src in enumerate((k_hbm, v_hbm)):
                load(src.at[pl.ds(t * part, part), lanes(i * head_dim, head_dim)],
                     kvout.at[i, t, z], 0)

    @pl.when(own)
    def _():
        for g2 in range(group):
            load(q_hbm.at[:, lanes((y * group + g2) * head_dim, head_dim)],
                 qbuf.at[y, pl.ds(g2 * rows, rows)], 1)
        for t in range(PARTS):
            for z, src in enumerate((k_hbm, v_hbm)):
                load(src.at[pl.ds(t * part, part), lanes(y * head_dim, head_dim)],
                     kvbuf.at[me, t, z], 1)

    order_copy = pltpu.make_async_copy(order_hbm, order, load_sem.at[2])
    order_copy.start()

    def wait(sem, count):
        @pl.when(count > 0)
        def _():
            pl.semaphore_wait(sem, count)

    wait(barrier, 2 * place + c + x + g * (2 + 4 * c))

    for m in range(TEAM):
        @pl.when(rank(m) < place)
        def _():
            signal(ready.at[me], g * TEAM + m, x * 2)
            signal(ready.at[me], g * TEAM + m, x * 2 + 1)

    @pl.when(c == 1)
    def _():
        signal(ready.at[me], me, partner)

        def answer_team(d):
            @pl.when(g - d >= 0)
            def _():
                for m in range(TEAM):
                    signal(ready.at[me], (g - d) * TEAM + m, x * 2 + keeper)

        loop(1, teams, answer_team)

    def q_copy(i):
        return pltpu.make_async_remote_copy(
            src_ref=qout.at[i], dst_ref=qbuf.at[y], send_sem=q_send, recv_sem=q_recv.at[y],
            device_id=(g * TEAM + base + i, x * 2 + keeper), device_id_type=MESH)

    def kv_copy(i, t, team, core, sem):
        return pltpu.make_async_remote_copy(
            src_ref=kvout.at[i, t], dst_ref=kvbuf.at[me, t],
            send_sem=sem, recv_sem=kv_recv.at[me, t],
            device_id=(team * TEAM + base + i, x * 2 + core), device_id_type=MESH)

    def share(slot, t):
        return pltpu.make_async_remote_copy(
            src_ref=kvbuf.at[slot, t], dst_ref=kvbuf.at[slot, t],
            send_sem=share_sem, recv_sem=kv_recv.at[slot, t],
            device_id=(me, partner), device_id_type=MESH)

    def ask(i):
        q_copy(i).start()

    def near(i):
        for t in range(PARTS):
            kv_copy(i, t, g, 0, near_sem).start()

    def cross(team):
        for i in range(2):
            for t in range(PARTS):
                kv_copy(i, t, team, 1, cross_sem).start()

    for i, whole in ((0, (qout, kvout)), ):
        for z in whole:
            pltpu.make_async_copy(z, z, load_sem.at[i]).wait()

    pair = [y, 1 - y]
    spot = [(1 - c) + 2 * i for i in pair]

    def cross_back(d):
        @pl.when(g - d >= 0)
        def _():
            cross(g - d)

    def cross_on(d):
        @pl.when(g + d < teams)
        def _():
            for i in range(2):
                pl.semaphore_wait(ready.at[(g + d) * TEAM + base + i], 1)
            cross(g + d)

    for i, r in zip(pair, spot):
        pl.when(r < place)(functools.partial(ask, i))
    loop(1, teams, cross_back)
    for i, r in zip(pair, spot):
        pl.when(r < place)(functools.partial(near, i))

    for i, r in zip(pair, spot):
        @pl.when(r > place)
        def _():
            pl.semaphore_wait(ready.at[g * TEAM + base + i], 2)
            ask(i)

    for i, r in zip(pair, spot):
        pl.when(r > place)(functools.partial(near, i))

    @pl.when(c == 0)
    def _():
        pl.semaphore_wait(ready.at[me], 1)

    @pl.when(own)
    def _():
        for z in (qbuf.at[0], kvbuf.at[0]):
            pltpu.make_async_copy(z, z, load_sem.at[1]).wait()
        for t in range(PARTS):
            share(me, t).start()

    loop(1, teams, cross_on)

    maxima[...] = jnp.full_like(maxima, FLOOR)
    sums[...] = jnp.zeros_like(sums)
    accum[...] = jnp.zeros_like(accum)
    order_copy.wait()

    row = lax.broadcasted_iota(jnp.int32, (rows, rows), 0)
    col = lax.broadcasted_iota(jnp.int32, (rows, rows), 1)
    per = order.shape[0] // n
    blk = rows // per

    def placed(index, s):
        out = index + order[s * per] * blk
        for b in range(1, per):
            out = jnp.where(index >= b * blk, index + (order[s * per + b] - b) * blk, out)
        return out

    query_pos = [placed(row, g * TEAM + base + rs) for rs in range(2)]

    def fold(z):
        return z.reshape(rows, head_dim)

    def attend(parts, slots):
        for rs in parts:
            scores = []
            for slot in slots:
                one = lax.dot_general(
                    qbuf[rs], fold(kvbuf[slot, :, 0]), (((1,), (1,)), ((), ())),
                    preferred_element_type=jnp.float32) * scale
                allowed = placed(col, slot) <= query_pos[rs]
                scores.append(jnp.where(jnp.concatenate([allowed] * group, 0), one, MASKED))
            before = maxima[rs]
            top = functools.reduce(jnp.maximum, scores)
            fresh = jnp.maximum(before, jnp.max(top, axis=1, keepdims=True))
            factor = jnp.exp(before - fresh)
            maxima[rs] = fresh
            weights = [jnp.exp(one - fresh) for one in scores]
            sums[rs] = sums[rs] * factor + functools.reduce(jnp.add, weights)
            update = [
                lax.dot_general(
                    w.astype(jnp.bfloat16), fold(kvbuf[slot, :, 1]), (((1,), (0,)), ((), ())),
                    preferred_element_type=jnp.float32)
                for w, slot in zip(weights, slots)]
            accum[rs] = accum[rs] * jnp.concatenate(
                [factor] * (head_dim // rows), 1) + functools.reduce(jnp.add, update)

    def landed(slot, t):
        share(slot, t).wait_recv()

    def take(slot, core):
        for t in range(PARTS):
            landed(slot, t)

            @pl.when(c == core)
            def _():
                share(slot, t).start()
        return slot

    @pl.when(other)
    def _():
        for t in range(PARTS):
            landed(me, t)

    for rs in range(2):
        @pl.when(other | (y != rs))
        def _():
            pltpu.make_async_remote_copy(
                src_ref=qout.at[0], dst_ref=qbuf.at[rs], send_sem=q_send,
                recv_sem=q_recv.at[rs], device_id=(me, partner), device_id_type=MESH).wait_recv()

    attend((0, 1), (me,))

    beside = g * TEAM + j + 1 - 2 * y
    above = g * TEAM + lax.rem(j + 2, TEAM)
    across = above + 1 - 2 * y
    for m in range(TEAM):
        @pl.when((m // 2 == c) & (rank(m) > place))
        def _():
            pl.semaphore_wait(ready.at[g * TEAM + m], 2)

    for xx in range(planes):
        @pl.when(xx < x)
        def _():
            signal(plane_ready, me, xx * 2 + c)

    wait(plane_ready, planes - 1 - x)

    for xx in range(planes):
        @pl.when(xx > x)
        def _():
            signal(plane_ready, me, xx * 2 + c)

    def wait_for(slot):
        for t in range(PARTS):
            landed(slot, t)
        return slot

    def pass_on(slot):
        for t in range(PARTS):
            landed(slot, t)
            share(slot, t).start()
        return slot

    both = (0, 1)
    if teams == 2:
        there = (1 - g) * TEAM
        lead = jnp.where(y == 0, 2 * g, 2 - 2 * g)
        far = [there + lead, there + lead + 1, there + 2 - lead, there + 3 - lead]


        @pl.when(c == 0)
        def _():
            attend(both, (pass_on(beside),))
            attend(both, [wait_for(s) for s in far[:2]])

        @pl.when(c == 1)
        def _():
            for s in far[:2]:
                pass_on(s)
            attend(both, (wait_for(beside),))
            attend(both, far[:2])

        first = (g == 0) | (c == 0)
        way = jnp.where(first, 0, 1)
        close = (above, across)
        now = [jnp.where(first, a, b) for a, b in zip(close, far[2:])]
        final = [jnp.where(first, b, a) for a, b in zip(close, far[2:])]
        attend(both, [take(s, way) for s in now])
        for s in final:
            take(s, 1 - way)
    else:
        attend(both, [take(s, 0) for s in (beside, above, across)])

        def slot_of(k):
            return lax.rem(g + 1 + k // TEAM, teams) * TEAM + lax.rem(k, TEAM)

        def further(k):
            attend(both, (take(slot_of(jnp.int32(k)), 1),))

        loop(0, TEAM * (teams - 1) - 1, further)
        final = [slot_of(jnp.int32(TEAM * (teams - 1) - 1))]
        take(final[0], 1)

    def finish(rs):
        attend((rs,), final)
        total = jnp.sum(sums[rs], axis=1, keepdims=True)
        out = (accum[rs] / total).astype(jnp.bfloat16)
        for g2 in range(group):
            obuf[rs, :, g2 * head_dim:(g2 + 1) * head_dim] = out[g2 * rows:(g2 + 1) * rows]
        return jnp.log(total) + maxima[rs]

    columns = lanes(((x * 2 + keeper) * 2 + y) * width, width)
    wait(plane_ready, x)

    def send_out(rs):
        mine = own & (y == rs)
        for k in range(nh):
            to = lax.rem(x + 1 + k, planes) * 2 + lax.rem(c + 1 + k // planes, 2)
            src = obuf.at[rs, pl.ds(pl.multiple_of(to * keep, keep), keep)]

            def away():
                pltpu.make_async_remote_copy(
                    src_ref=src, dst_ref=attn.at[:, columns], send_sem=o_send, recv_sem=o_recv,
                    device_id=(g * TEAM + base + rs, to), device_id_type=MESH).start()

            if k < nh - 1:
                away()
            else:
                pl.when(jnp.logical_not(mine))(away)

                @pl.when(mine)
                def _():
                    pltpu.make_async_copy(src, attn.at[:, columns], o_send).start()

    def send_lse(rs, full):
        for g2 in range(group):
            lse_tx[rs, g2:g2 + 1, :] = jnp.transpose(full[g2 * rows:(g2 + 1) * rows])[:1]
        mine = own & (y == rs)

        @pl.when(jnp.logical_not(mine))
        def _():
            pltpu.make_async_remote_copy(
                src_ref=lse_tx.at[rs], dst_ref=lse_rx.at[y], send_sem=l_send, recv_sem=l_recv,
                device_id=(g * TEAM + base + rs, x * 2 + keeper), device_id_type=MESH).start()

        @pl.when(mine)
        def _():
            lse_rx[rs] = lse_tx[rs]

    fulls = []
    for rs in range(2):
        fulls.append(finish(rs))
        send_out(rs)
    for rs in range(2):
        send_lse(rs, fulls[rs])

    def drain(ref, sem):
        pltpu.make_async_copy(ref, ref, sem).wait()

    def by_kind(ref, less, sem):
        pl.when(own)(lambda: drain(less, sem))
        pl.when(other)(lambda: drain(ref, sem))

    by_kind(lse_rx, lse_rx.at[pl.ds(0, 1)], l_recv)
    lse[...] = jnp.concatenate([lse_rx[0, :group], lse_rx[1, :group]], 0)
    by_kind(attn, attn.at[:, pl.ds(0, (2 * nh - 1) * width)], o_recv)
    drain(attn, o_send)
    by_kind(lse_tx, lse_tx.at[pl.ds(0, 1)], l_send)
    by_kind(qbuf, qbuf.at[pl.ds(0, 1)], q_send)
    by_kind(kvbuf.at[pl.ds(0, 2)], kvbuf.at[pl.ds(0, 1)], near_sem)
    drain(kvbuf.at[pl.ds(0, 2 * (teams - 1))], cross_sem)
    for core, count in ((0, TEAM - 1), (1, TEAM * (teams - 1))):
        pl.when((c == core) & own)(
            functools.partial(drain, kvbuf.at[pl.ds(0, count + 1)], share_sem))
        pl.when((c == core) & other)(
            functools.partial(drain, kvbuf.at[pl.ds(0, count)], share_sem))


def hand_over(attn, lse, attn_hbm, lse_hbm, sem):
    copies = [
        pltpu.make_async_copy(attn, attn_hbm, sem.at[0]),
        pltpu.make_async_copy(lse, lse_hbm, sem.at[1]),
    ]
    for c in copies:
        c.start()
    for c in copies:
        c.wait()


def local(n, nh, queries, keys, values, block_order):
    rows = queries.shape[0]
    head_dim, group = HEAD_SIZE, QUERY_GROUP
    high = group * rows
    bf16, f32 = jnp.bfloat16, jnp.float32
    dma = pltpu.SemaphoreType.DMA
    attn, lse = pl.pallas_call(
        functools.partial(kernel, n, nh),
        out_shape=(
            pltpu.VMEM((rows // nh, queries.shape[1] * nh), bf16),
            pltpu.VMEM((2 * group, rows), f32),
        ),
        in_specs=[pl.BlockSpec(memory_space=pl.ANY)] * 4,
        out_specs=(pl.BlockSpec(memory_space=pltpu.VMEM),) * 2,
        scratch_shapes=[
            pltpu.VMEM((2, high, head_dim), bf16),
            pltpu.VMEM((2, high, head_dim), bf16),
            pltpu.VMEM((2, PARTS, 2, rows // PARTS, head_dim), bf16),
            pltpu.VMEM((n, PARTS, 2, rows // PARTS, head_dim), bf16),
            pltpu.VMEM((2, high, rows), f32),
            pltpu.VMEM((2, high, rows), f32),
            pltpu.VMEM((2, high, head_dim), f32),
            pltpu.VMEM((2, rows, group * head_dim), bf16),
            pltpu.VMEM((2, 8, rows), f32),
            pltpu.VMEM((2, 8, rows), f32),
            pltpu.SMEM(block_order.shape, jnp.int32),
            dma((3,)),
            dma,
            dma,
            dma,
            dma((n, PARTS)),
            dma,
            dma((2,)),
            dma,
            dma,
            dma,
            dma,
            pltpu.SemaphoreType.REGULAR((n,)),
            pltpu.SemaphoreType.REGULAR,
        ],
        compiler_params=pltpu.CompilerParams(collective_id=0, has_side_effects=True),
    )(block_order, queries, keys, values)
    attn, lse = (pltpu.with_memory_space_constraint(z, pltpu.VMEM) for z in (attn, lse))
    return pl.pallas_call(
        hand_over,
        out_shape=(pltpu.HBM(attn.shape, bf16), pltpu.HBM(lse.shape, f32)),
        in_specs=[pl.BlockSpec(memory_space=pltpu.VMEM)] * 2,
        out_specs=(pl.BlockSpec(memory_space=pltpu.HBM),) * 2,
        scratch_shapes=[dma((2,))],
    )(attn, lse)


def solution(mesh):
    in_specs = (P("seq", "head"), P("seq", "head"), P("seq", "head"), P())
    out_specs = (P(("seq", "head"), None), P("head", "seq"))
    body = functools.partial(local, mesh.shape["seq"], mesh.shape["head"])
    return jax.shard_map(body, mesh=mesh, in_specs=in_specs, out_specs=out_specs, check_vma=False)
```

time: 28.9 us -> 27.7 us (0.958)
  the two profiles are of different devices: /device:TPU:0 before, /device:TPU:25 now
where the time goes in v2:
time: 27.7 us; the launch traced here: 27.5 us
  Pallas kernels  26.9 us (97%)
  between operations  0.64 us (2%)
    pallas_call x1, Pallas kernels, local(): pl.pallas_call(functools.partial(kernel, n, nh), out_shape=(pltpu.VMEM((r...  26.2 us
    pallas_call x1, Pallas kernels, local(): pl.pallas_call(hand_over, out_shape=(pltpu.HBM(attn.shape, bf16), pltpu.H...  0.72 us

profile of v2, /device:TPU:25, one launch (start us, length us, event | category | flops | bytes accessed | tf_op | source)
XLA Modules:
  0.0 27.5 jit_solution(3494118617422328890)
XLA Ops:
  0.6 26.2 %shard_map.59 = (bf16[32,4096]{1,0:T(8,128)(2,1)S(1)}, f32[4,128]{1,0:T(4,128)S(1)}) custom-call(s32[16]{0:T(128)} %order_hbm.1, bf16[128,1024]{1,0:T(8,128)(2,1)} %q_hbm.1, bf16[128,512]{1,0:T(8,128)(2,1)} %k_hbm.1, bf16[128,512]{1,0:T(8,128)(2,1)} %v_hbm.1), custom_call_target="tpu_custom_call" | custom-call | tf_op jit(solution)/shard_map/pallas_call | solution.py:454
  26.8 0.7 %shard_map.60 = (bf16[32,4096]{1,0:T(8,128)(2,1)}, f32[4,128]{1,0:T(4,128)}) custom-call(bf16[32,4096]{1,0:T(8,128)(2,1)S(1)} %get-tuple-element.4.attn, f32[4,128]{1,0:T(4,128)S(1)} %get-tuple-element.5.lse), custom_call_target="tpu_custom_call" | custom-call | tf_op jit(solution)/shard_map/pallas_call | solution.py:491

commit v3 on v2

--- a/solution.py
+++ b/solution.py
@@ -189,20 +189,19 @@
                 pl.semaphore_wait(ready.at[(g + d) * TEAM + base + i], 1)
             cross(g + d)
 
+    def ask_both():
+        for i, r in zip(pair, spot):
+            @pl.when(r > place)
+            def _():
+                pl.semaphore_wait(ready.at[g * TEAM + base + i], 2)
+
+            pl.when(r != place)(functools.partial(ask, i))
+
+    pl.when(spot[0] < place)(ask_both)
+    loop(1, teams, cross_back)
+    pl.when(spot[0] >= place)(ask_both)
     for i, r in zip(pair, spot):
-        pl.when(r < place)(functools.partial(ask, i))
-    loop(1, teams, cross_back)
-    for i, r in zip(pair, spot):
-        pl.when(r < place)(functools.partial(near, i))
-
-    for i, r in zip(pair, spot):
-        @pl.when(r > place)
-        def _():
-            pl.semaphore_wait(ready.at[g * TEAM + base + i], 2)
-            ask(i)
-
-    for i, r in zip(pair, spot):
-        pl.when(r > place)(functools.partial(near, i))
+        pl.when(r != place)(functools.partial(near, i))
 
     @pl.when(c == 0)
     def _():
@@ -301,13 +300,6 @@
         def _():
             signal(plane_ready, me, xx * 2 + c)
 
-    wait(plane_ready, planes - 1 - x)
-
-    for xx in range(planes):
-        @pl.when(xx > x)
-        def _():
-            signal(plane_ready, me, xx * 2 + c)
-
     def wait_for(slot):
         for t in range(PARTS):
             landed(slot, t)
@@ -322,6 +314,7 @@
     both = (0, 1)
     if teams == 2:
         there = (1 - g) * TEAM
+        close = (above, across)
         lead = jnp.where(y == 0, 2 * g, 2 - 2 * g)
         far = [there + lead, there + lead + 1, there + 2 - lead, there + 3 - lead]
 
@@ -329,7 +322,7 @@
         @pl.when(c == 0)
         def _():
             attend(both, (pass_on(beside),))
-            attend(both, [wait_for(s) for s in far[:2]])
+            attend(both, [pass_on(s) for s in close])
 
         @pl.when(c == 1)
         def _():
@@ -338,16 +331,26 @@
             attend(both, (wait_for(beside),))
             attend(both, far[:2])
 
-        first = (g == 0) | (c == 0)
-        way = jnp.where(first, 0, 1)
-        close = (above, across)
-        now = [jnp.where(first, a, b) for a, b in zip(close, far[2:])]
-        final = [jnp.where(first, b, a) for a, b in zip(close, far[2:])]
-        attend(both, [take(s, way) for s in now])
+        now = [jnp.where(c == 0, a, b) for a, b in zip(far[:2], far[2:])]
+        final = [jnp.where(c == 0, a, b) for a, b in zip(far[2:], close)]
+        wait(plane_ready, planes - 1 - x)
+
+        for xx in range(planes):
+            @pl.when(xx > x)
+            def _():
+                signal(plane_ready, me, xx * 2 + c)
+
+        attend(both, [take(s, 1) for s in now])
         for s in final:
-            take(s, 1 - way)
+            wait_for(s)
     else:
         attend(both, [take(s, 0) for s in (beside, above, across)])
+        wait(plane_ready, planes - 1 - x)
+
+        for xx in range(planes):
+            @pl.when(xx > x)
+            def _():
+                signal(plane_ready, me, xx * 2 + c)
 
         def slot_of(k):
             return lax.rem(g + 1 + k // TEAM, teams) * TEAM + lax.rem(k, TEAM)

time: 27.7 us -> 26 us (0.939)
  the two profiles are of different devices: /device:TPU:25 before, /device:TPU:0 now
where the time goes in v3:
time: 26 us; the launch traced here: 25.8 us
  Pallas kernels  25.1 us (97%)
  between operations  0.64 us (2%)
    pallas_call x1, Pallas kernels, local(): pl.pallas_call(functools.partial(kernel, n, nh), out_shape=(pltpu.VMEM((r...  24.4 us
    pallas_call x1, Pallas kernels, local(): pl.pallas_call(hand_over, out_shape=(pltpu.HBM(attn.shape, bf16), pltpu.H...  0.72 us

profile of v3, /device:TPU:0, one launch (start us, length us, event | category | flops | bytes accessed | tf_op | source)
XLA Modules:
  0.0 25.8 jit_solution(8404291264859677902)
XLA Ops:
  0.6 24.4 %shard_map.59 = (bf16[32,4096]{1,0:T(8,128)(2,1)S(1)}, f32[4,128]{1,0:T(4,128)S(1)}) custom-call(s32[16]{0:T(128)} %order_hbm.1, bf16[128,1024]{1,0:T(8,128)(2,1)} %q_hbm.1, bf16[128,512]{1,0:T(8,128)(2,1)} %k_hbm.1, bf16[128,512]{1,0:T(8,128)(2,1)} %v_hbm.1), custom_call_target="tpu_custom_call" | custom-call | tf_op jit(solution)/shard_map/pallas_call | solution.py:457
  25.1 0.7 %shard_map.60 = (bf16[32,4096]{1,0:T(8,128)(2,1)}, f32[4,128]{1,0:T(4,128)}) custom-call(bf16[32,4096]{1,0:T(8,128)(2,1)S(1)} %get-tuple-element.4.attn, f32[4,128]{1,0:T(4,128)S(1)} %get-tuple-element.5.lse), custom_call_target="tpu_custom_call" | custom-call | tf_op jit(solution)/shard_map/pallas_call | solution.py:494

commit v4 on v3

--- a/solution.py
+++ b/solution.py
@@ -41,10 +41,10 @@
     x, c = h // 2, lax.rem(h, 2)
     g, j = me // TEAM, lax.rem(me, TEAM)
     y = lax.rem(j, 2)
-    keeper = 1 - j // 2
+    keeper = 1 - y
     own = c == keeper
     other = jnp.logical_not(own)
-    base = 2 * (1 - c)
+    base = 1 - c
     partner = x * 2 + 1 - c
     upper = j // 2
 
@@ -72,7 +72,7 @@
         @pl.when(g + d < teams)
         def _():
             for i in range(2):
-                signal(barrier, (g + d) * TEAM + base + i, x * 2 + 1)
+                signal(barrier, (g + d) * TEAM + base + 2 * i, x * 2 + 1)
 
             @pl.when(c == 1)
             def _():
@@ -106,11 +106,11 @@
     @pl.when(own)
     def _():
         for g2 in range(group):
-            load(q_hbm.at[:, lanes((y * group + g2) * head_dim, head_dim)],
-                 qbuf.at[y, pl.ds(g2 * rows, rows)], 1)
+            load(q_hbm.at[:, lanes((upper * group + g2) * head_dim, head_dim)],
+                 qbuf.at[upper, pl.ds(g2 * rows, rows)], 1)
         for t in range(PARTS):
             for z, src in enumerate((k_hbm, v_hbm)):
-                load(src.at[pl.ds(t * part, part), lanes(y * head_dim, head_dim)],
+                load(src.at[pl.ds(t * part, part), lanes(upper * head_dim, head_dim)],
                      kvbuf.at[me, t, z], 1)
 
     order_copy = pltpu.make_async_copy(order_hbm, order, load_sem.at[2])
@@ -143,14 +143,14 @@
 
     def q_copy(i):
         return pltpu.make_async_remote_copy(
-            src_ref=qout.at[i], dst_ref=qbuf.at[y], send_sem=q_send, recv_sem=q_recv.at[y],
-            device_id=(g * TEAM + base + i, x * 2 + keeper), device_id_type=MESH)
+            src_ref=qout.at[i], dst_ref=qbuf.at[upper], send_sem=q_send, recv_sem=q_recv.at[upper],
+            device_id=(g * TEAM + base + 2 * i, x * 2 + keeper), device_id_type=MESH)
 
     def kv_copy(i, t, team, core, sem):
         return pltpu.make_async_remote_copy(
             src_ref=kvout.at[i, t], dst_ref=kvbuf.at[me, t],
             send_sem=sem, recv_sem=kv_recv.at[me, t],
-            device_id=(team * TEAM + base + i, x * 2 + core), device_id_type=MESH)
+            device_id=(team * TEAM + base + 2 * i, x * 2 + core), device_id_type=MESH)
 
     def share(slot, t):
         return pltpu.make_async_remote_copy(
@@ -163,10 +163,10 @@
 
     def near(i):
         for t in range(PARTS):
-            kv_copy(i, t, g, 0, near_sem).start()
-
-    def cross(team):
-        for i in range(2):
+            kv_copy(i, t, g, 1, near_sem).start()
+
+    def cross(team, turn):
+        for i in turn:
             for t in range(PARTS):
                 kv_copy(i, t, team, 1, cross_sem).start()
 
@@ -174,32 +174,32 @@
         for z in whole:
             pltpu.make_async_copy(z, z, load_sem.at[i]).wait()
 
-    pair = [y, 1 - y]
-    spot = [(1 - c) + 2 * i for i in pair]
+    pair = [upper, 1 - upper]
+    spot = [i + 2 * base for i in pair]
 
     def cross_back(d):
         @pl.when(g - d >= 0)
         def _():
-            cross(g - d)
+            cross(g - d, (0, 1))
 
     def cross_on(d):
         @pl.when(g + d < teams)
         def _():
             for i in range(2):
-                pl.semaphore_wait(ready.at[(g + d) * TEAM + base + i], 1)
-            cross(g + d)
+                pl.semaphore_wait(ready.at[(g + d) * TEAM + base + 2 * i], 1)
+            cross(g + d, (1, 0))
 
     def ask_both():
         for i, r in zip(pair, spot):
             @pl.when(r > place)
             def _():
-                pl.semaphore_wait(ready.at[g * TEAM + base + i], 2)
+                pl.semaphore_wait(ready.at[g * TEAM + base + 2 * i], 2)
 
             pl.when(r != place)(functools.partial(ask, i))
 
-    pl.when(spot[0] < place)(ask_both)
+    pl.when(spot[1] < place)(ask_both)
     loop(1, teams, cross_back)
-    pl.when(spot[0] >= place)(ask_both)
+    pl.when(spot[1] >= place)(ask_both)
     for i, r in zip(pair, spot):
         pl.when(r != place)(functools.partial(near, i))
 
@@ -232,7 +232,7 @@
             out = jnp.where(index >= b * blk, index + (order[s * per + b] - b) * blk, out)
         return out
 
-    query_pos = [placed(row, g * TEAM + base + rs) for rs in range(2)]
+    query_pos = [placed(row, g * TEAM + base + 2 * rs) for rs in range(2)]
 
     def fold(z):
         return z.reshape(rows, head_dim)
@@ -264,11 +264,11 @@
     def landed(slot, t):
         share(slot, t).wait_recv()
 
-    def take(slot, core):
+    def take(slot):
         for t in range(PARTS):
             landed(slot, t)
 
-            @pl.when(c == core)
+            @pl.when(c == 1)
             def _():
                 share(slot, t).start()
         return slot
@@ -279,7 +279,7 @@
             landed(me, t)
 
     for rs in range(2):
-        @pl.when(other | (y != rs))
+        @pl.when(other | (upper != rs))
         def _():
             pltpu.make_async_remote_copy(
                 src_ref=qout.at[0], dst_ref=qbuf.at[rs], send_sem=q_send,
@@ -291,7 +291,7 @@
     above = g * TEAM + lax.rem(j + 2, TEAM)
     across = above + 1 - 2 * y
     for m in range(TEAM):
-        @pl.when((m // 2 == c) & (rank(m) > place))
+        @pl.when((m % 2 == c) & (rank(m) > place))
         def _():
             pl.semaphore_wait(ready.at[g * TEAM + m], 2)
 
@@ -299,40 +299,21 @@
         @pl.when(xx < x)
         def _():
             signal(plane_ready, me, xx * 2 + c)
-
-    def wait_for(slot):
-        for t in range(PARTS):
-            landed(slot, t)
-        return slot
-
-    def pass_on(slot):
-        for t in range(PARTS):
-            landed(slot, t)
-            share(slot, t).start()
-        return slot
 
     both = (0, 1)
     if teams == 2:
         there = (1 - g) * TEAM
         close = (above, across)
-        lead = jnp.where(y == 0, 2 * g, 2 - 2 * g)
+        lead = 2 * upper
         far = [there + lead, there + lead + 1, there + 2 - lead, there + 3 - lead]
 
 
-        @pl.when(c == 0)
-        def _():
-            attend(both, (pass_on(beside),))
-            attend(both, [pass_on(s) for s in close])
-
-        @pl.when(c == 1)
-        def _():
-            for s in far[:2]:
-                pass_on(s)
-            attend(both, (wait_for(beside),))
-            attend(both, far[:2])
-
-        now = [jnp.where(c == 0, a, b) for a, b in zip(far[:2], far[2:])]
-        final = [jnp.where(c == 0, a, b) for a, b in zip(far[2:], close)]
+        attend(both, (take(beside),))
+        lower = g == 0
+        stages = [(jnp.where(lower, a, b), jnp.where(lower, b, d), jnp.where(lower, d, a))
+                  for a, b, d in zip(close, far[:2], far[2:])]
+        first, second, final = zip(*stages)
+        attend(both, [take(s) for s in first])
         wait(plane_ready, planes - 1 - x)
 
         for xx in range(planes):
@@ -340,11 +321,11 @@
             def _():
                 signal(plane_ready, me, xx * 2 + c)
 
-        attend(both, [take(s, 1) for s in now])
+        attend(both, [take(s) for s in second])
         for s in final:
-            wait_for(s)
+            take(s)
     else:
-        attend(both, [take(s, 0) for s in (beside, above, across)])
+        attend(both, [take(s) for s in (beside, above, across)])
         wait(plane_ready, planes - 1 - x)
 
         for xx in range(planes):
@@ -356,64 +337,64 @@
             return lax.rem(g + 1 + k // TEAM, teams) * TEAM + lax.rem(k, TEAM)
 
         def further(k):
-            attend(both, (take(slot_of(jnp.int32(k)), 1),))
+            attend(both, (take(slot_of(jnp.int32(k))),))
 
         loop(0, TEAM * (teams - 1) - 1, further)
         final = [slot_of(jnp.int32(TEAM * (teams - 1) - 1))]
-        take(final[0], 1)
+        take(final[0])
 
     def finish(rs):
-        attend((rs,), final)
         total = jnp.sum(sums[rs], axis=1, keepdims=True)
         out = (accum[rs] / total).astype(jnp.bfloat16)
         for g2 in range(group):
             obuf[rs, :, g2 * head_dim:(g2 + 1) * head_dim] = out[g2 * rows:(g2 + 1) * rows]
         return jnp.log(total) + maxima[rs]
 
-    columns = lanes(((x * 2 + keeper) * 2 + y) * width, width)
+    columns = lanes(((x * 2 + keeper) * 2 + upper) * width, width)
     wait(plane_ready, x)
 
-    def send_out(rs):
-        mine = own & (y == rs)
-        for k in range(nh):
-            to = lax.rem(x + 1 + k, planes) * 2 + lax.rem(c + 1 + k // planes, 2)
-            src = obuf.at[rs, pl.ds(pl.multiple_of(to * keep, keep), keep)]
-
-            def away():
-                pltpu.make_async_remote_copy(
-                    src_ref=src, dst_ref=attn.at[:, columns], send_sem=o_send, recv_sem=o_recv,
-                    device_id=(g * TEAM + base + rs, to), device_id_type=MESH).start()
-
-            if k < nh - 1:
-                away()
-            else:
-                pl.when(jnp.logical_not(mine))(away)
-
-                @pl.when(mine)
-                def _():
-                    pltpu.make_async_copy(src, attn.at[:, columns], o_send).start()
+    def send_out(rs, k):
+        mine = own & (upper == rs)
+        to = lax.rem(x + 1 + k, planes) * 2 + lax.rem(c + 1 + k // planes, 2)
+        src = obuf.at[rs, pl.ds(pl.multiple_of(to * keep, keep), keep)]
+
+        def away():
+            pltpu.make_async_remote_copy(
+                src_ref=src, dst_ref=attn.at[:, columns], send_sem=o_send, recv_sem=o_recv,
+                device_id=(g * TEAM + base + 2 * rs, to), device_id_type=MESH).start()
+
+        if k < nh - 1:
+            away()
+        else:
+            pl.when(jnp.logical_not(mine))(away)
+
+            @pl.when(mine)
+            def _():
+                pltpu.make_async_copy(src, attn.at[:, columns], o_send).start()
 
     def send_lse(rs, full):
         for g2 in range(group):
             lse_tx[rs, g2:g2 + 1, :] = jnp.transpose(full[g2 * rows:(g2 + 1) * rows])[:1]
-        mine = own & (y == rs)
+        mine = own & (upper == rs)
 
         @pl.when(jnp.logical_not(mine))
         def _():
             pltpu.make_async_remote_copy(
-                src_ref=lse_tx.at[rs], dst_ref=lse_rx.at[y], send_sem=l_send, recv_sem=l_recv,
-                device_id=(g * TEAM + base + rs, x * 2 + keeper), device_id_type=MESH).start()
+                src_ref=lse_tx.at[rs], dst_ref=lse_rx.at[upper], send_sem=l_send, recv_sem=l_recv,
+                device_id=(g * TEAM + base + 2 * rs, x * 2 + keeper), device_id_type=MESH).start()
 
         @pl.when(mine)
         def _():
             lse_rx[rs] = lse_tx[rs]
 
-    fulls = []
-    for rs in range(2):
-        fulls.append(finish(rs))
-        send_out(rs)
-    for rs in range(2):
-        send_lse(rs, fulls[rs])
+    attend(both, final)
+    fulls = [finish(0), finish(1)]
+    for k in range(nh):
+        for rs in (1 - upper, upper):
+            send_out(rs, k)
+        if k == 1:
+            for rs in range(2):
+                send_lse(rs, fulls[rs])
 
     def drain(ref, sem):
         pltpu.make_async_copy(ref, ref, sem).wait()
@@ -430,11 +411,9 @@
     by_kind(qbuf, qbuf.at[pl.ds(0, 1)], q_send)
     by_kind(kvbuf.at[pl.ds(0, 2)], kvbuf.at[pl.ds(0, 1)], near_sem)
     drain(kvbuf.at[pl.ds(0, 2 * (teams - 1))], cross_sem)
-    for core, count in ((0, TEAM - 1), (1, TEAM * (teams - 1))):
-        pl.when((c == core) & own)(
-            functools.partial(drain, kvbuf.at[pl.ds(0, count + 1)], share_sem))
-        pl.when((c == core) & other)(
-            functools.partial(drain, kvbuf.at[pl.ds(0, count)], share_sem))
+    pl.when((c == 1) & own)(functools.partial(drain, kvbuf, share_sem))
+    pl.when((c == 1) & other)(functools.partial(drain, kvbuf.at[pl.ds(0, n - 1)], share_sem))
+    pl.when((c == 0) & own)(functools.partial(drain, kvbuf.at[0], share_sem))
 
 
 def hand_over(attn, lse, attn_hbm, lse_hbm, sem):

time: 26 us -> 24.8 us (0.954)
  the two profiles are of different devices: /device:TPU:0 before, /device:TPU:28 now
where the time goes in v4:
time: 24.8 us; the launch traced here: 24.6 us
  Pallas kernels  24 us (97%)
  between operations  0.64 us (3%)
    pallas_call x1, Pallas kernels, local(): pl.pallas_call(functools.partial(kernel, n, nh), out_shape=(pltpu.VMEM((r...  23.3 us
    pallas_call x1, Pallas kernels, local(): pl.pallas_call(hand_over, out_shape=(pltpu.HBM(attn.shape, bf16), pltpu.H...  0.72 us

profile of v4, /device:TPU:28, one launch (start us, length us, event | category | flops | bytes accessed | tf_op | source)
XLA Modules:
  0.0 24.6 jit_solution(17770615939941089887)
XLA Ops:
  0.6 23.3 %shard_map.59 = (bf16[32,4096]{1,0:T(8,128)(2,1)S(1)}, f32[4,128]{1,0:T(4,128)S(1)}) custom-call(s32[16]{0:T(128)} %order_hbm.1, bf16[128,1024]{1,0:T(8,128)(2,1)} %q_hbm.1, bf16[128,512]{1,0:T(8,128)(2,1)} %k_hbm.1, bf16[128,512]{1,0:T(8,128)(2,1)} %v_hbm.1), custom_call_target="tpu_custom_call" | custom-call | tf_op jit(solution)/shard_map/pallas_call | solution.py:436
  23.9 0.7 %shard_map.60 = (bf16[32,4096]{1,0:T(8,128)(2,1)}, f32[4,128]{1,0:T(4,128)}) custom-call(bf16[32,4096]{1,0:T(8,128)(2,1)S(1)} %get-tuple-element.4.attn, f32[4,128]{1,0:T(4,128)S(1)} %get-tuple-element.5.lse), custom_call_target="tpu_custom_call" | custom-call | tf_op jit(solution)/shard_map/pallas_call | solution.py:473

commit v5 on v4

--- a/solution.py
+++ b/solution.py
@@ -11,7 +11,8 @@
 QUERY_GROUP = 2
 MASKED = -1e30
 FLOOR = -1e20
-PARTS = 1
+PARTS = 2
+LEAD = 1
 TEAM = 4
 MESH = pl.DeviceIdType.MESH
 
@@ -185,9 +186,11 @@
     def cross_on(d):
         @pl.when(g + d < teams)
         def _():
-            for i in range(2):
-                pl.semaphore_wait(ready.at[(g + d) * TEAM + base + 2 * i], 1)
-            cross(g + d, (1, 0))
+            for i, spans in ((0, range(LEAD)), (1, range(PARTS)), (0, range(LEAD, PARTS))):
+                if spans.start == 0:
+                    pl.semaphore_wait(ready.at[(g + d) * TEAM + base + 2 * i], 1)
+                for t in spans:
+                    kv_copy(i, t, g + d, 1, cross_sem).start()
 
     def ask_both():
         for i, r in zip(pair, spot):
@@ -309,9 +312,12 @@
 
 
         attend(both, (take(beside),))
-        lower = g == 0
-        stages = [(jnp.where(lower, a, b), jnp.where(lower, b, d), jnp.where(lower, d, a))
-                  for a, b, d in zip(close, far[:2], far[2:])]
+        low, up = g == 0, upper == 1
+        stages = [
+            (jnp.where(low & up, a, b),
+             jnp.where(low & up, b, jnp.where(low | up, d, a)),
+             jnp.where(low == up, d, a))
+            for a, b, d in zip(close, far[:2], far[2:])]
         first, second, final = zip(*stages)
         attend(both, [take(s) for s in first])
         wait(plane_ready, planes - 1 - x)
@@ -388,13 +394,11 @@
             lse_rx[rs] = lse_tx[rs]
 
     attend(both, final)
-    fulls = [finish(0), finish(1)]
-    for k in range(nh):
-        for rs in (1 - upper, upper):
+    for rs in (1 - upper, upper):
+        full = finish(rs)
+        for k in range(nh):
             send_out(rs, k)
-        if k == 1:
-            for rs in range(2):
-                send_lse(rs, fulls[rs])
+        send_lse(rs, full)
 
     def drain(ref, sem):
         pltpu.make_async_copy(ref, ref, sem).wait()

time: 24.8 us -> 24.5 us (0.988)
  the two profiles are of different devices: /device:TPU:28 before, /device:TPU:0 now
where the time goes in v5:
time: 24.5 us; the launch traced here: 24.1 us
  Pallas kernels  23.5 us (96%)
  between operations  0.64 us (3%)
    pallas_call x1, Pallas kernels, local(): pl.pallas_call(functools.partial(kernel, n, nh), out_shape=(pltpu.VMEM((r...  22.8 us
    pallas_call x1, Pallas kernels, local(): pl.pallas_call(hand_over, out_shape=(pltpu.HBM(attn.shape, bf16), pltpu.H...  0.72 us

profile of v5, /device:TPU:0, one launch (start us, length us, event | category | flops | bytes accessed | tf_op | source)
XLA Modules:
  0.0 24.1 jit_solution(6684081513494993847)
XLA Ops:
  0.6 22.8 %shard_map.59 = (bf16[32,4096]{1,0:T(8,128)(2,1)S(1)}, f32[4,128]{1,0:T(4,128)S(1)}) custom-call(s32[16]{0:T(128)} %order_hbm.1, bf16[128,1024]{1,0:T(8,128)(2,1)} %q_hbm.1, bf16[128,512]{1,0:T(8,128)(2,1)} %k_hbm.1, bf16[128,512]{1,0:T(8,128)(2,1)} %v_hbm.1), custom_call_target="tpu_custom_call" | custom-call | tf_op jit(solution)/shard_map/pallas_call | solution.py:440
  23.4 0.7 %shard_map.60 = (bf16[32,4096]{1,0:T(8,128)(2,1)}, f32[4,128]{1,0:T(4,128)}) custom-call(bf16[32,4096]{1,0:T(8,128)(2,1)S(1)} %get-tuple-element.4.attn, f32[4,128]{1,0:T(4,128)S(1)} %get-tuple-element.5.lse), custom_call_target="tpu_custom_call" | custom-call | tf_op jit(solution)/shard_map/pallas_call | solution.py:477

commit v6 on v5

--- a/solution.py
+++ b/solution.py
@@ -351,7 +351,7 @@
 
     def finish(rs):
         total = jnp.sum(sums[rs], axis=1, keepdims=True)
-        out = (accum[rs] / total).astype(jnp.bfloat16)
+        out = (accum[rs] * (1.0 / total)).astype(jnp.bfloat16)
         for g2 in range(group):
             obuf[rs, :, g2 * head_dim:(g2 + 1) * head_dim] = out[g2 * rows:(g2 + 1) * rows]
         return jnp.log(total) + maxima[rs]
@@ -421,10 +421,11 @@
 
 
 def hand_over(attn, lse, attn_hbm, lse_hbm, sem):
-    copies = [
-        pltpu.make_async_copy(attn, attn_hbm, sem.at[0]),
-        pltpu.make_async_copy(lse, lse_hbm, sem.at[1]),
-    ]
+    step = attn.shape[1] // 4
+    copies = [pltpu.make_async_copy(lse, lse_hbm, sem.at[0])]
+    for i in range(4):
+        part = (slice(None), pl.ds(i * step, step))
+        copies.append(pltpu.make_async_copy(attn.at[part], attn_hbm.at[part], sem.at[1 + i]))
     for c in copies:
         c.start()
     for c in copies:
@@ -479,7 +480,7 @@
         out_shape=(pltpu.HBM(attn.shape, bf16), pltpu.HBM(lse.shape, f32)),
         in_specs=[pl.BlockSpec(memory_space=pltpu.VMEM)] * 2,
         out_specs=(pl.BlockSpec(memory_space=pltpu.HBM),) * 2,
-        scratch_shapes=[dma((2,))],
+        scratch_shapes=[dma((5,))],
     )(attn, lse)
 
 

time: 24.5 us -> 24.5 us (level)
  no operation moved by 1% of the time
where the time goes in v6:
time: 24.5 us; the launch traced here: 24.1 us
  Pallas kernels  23.5 us (96%)
  between operations  0.64 us (3%)
    pallas_call x1, Pallas kernels, local(): pl.pallas_call(functools.partial(kernel, n, nh), out_shape=(pltpu.VMEM((r...  22.8 us
    pallas_call x1, Pallas kernels, local(): pl.pallas_call(hand_over, out_shape=(pltpu.HBM(attn.shape, bf16), pltpu.H...  0.74 us

profile of v6, /device:TPU:0, one launch (start us, length us, event | category | flops | bytes accessed | tf_op | source)
XLA Modules:
  0.0 24.1 jit_solution(16414217146557530913)
XLA Ops:
  0.6 22.8 %shard_map.59 = (bf16[32,4096]{1,0:T(8,128)(2,1)S(1)}, f32[4,128]{1,0:T(4,128)S(1)}) custom-call(s32[16]{0:T(128)} %order_hbm.1, bf16[128,1024]{1,0:T(8,128)(2,1)} %q_hbm.1, bf16[128,512]{1,0:T(8,128)(2,1)} %k_hbm.1, bf16[128,512]{1,0:T(8,128)(2,1)} %v_hbm.1), custom_call_target="tpu_custom_call" | custom-call | tf_op jit(solution)/shard_map/pallas_call | solution.py:441
  23.4 0.7 %shard_map.60 = (bf16[32,4096]{1,0:T(8,128)(2,1)}, f32[4,128]{1,0:T(4,128)}) custom-call(bf16[32,4096]{1,0:T(8,128)(2,1)S(1)} %get-tuple-element.4.attn, f32[4,128]{1,0:T(4,128)S(1)} %get-tuple-element.5.lse), custom_call_target="tpu_custom_call" | custom-call | tf_op jit(solution)/shard_map/pallas_call | solution.py:478
